TPU v7x, 32 devices: a whole 2x2x4 slice. The times are simulated.
32 devices in a mesh: dom: 8 (over z, y), sub: 4 (over x, core).
Axes of the slice: x: 2, y: 2, z: 4, core: 2. Of those that a mesh axis runs over, the one named last changes fastest.
Arguments:
- node_state: bfloat16 [64, 32768], P(None, ('dom', 'sub')), may hold values from -6 to 6
- edge_state: bfloat16 [64, 98304], P(None, ('dom', 'sub')), may hold values from -6 to 6
- senders: int32 [98304], P(('dom', 'sub')), may hold values from 0 to 2559, as said below
- receivers: int32 [98304], P(('dom', 'sub')), may hold values from 0 to 1023
- send_index: int32 [32, 12, 128], P(('dom', 'sub')), may hold values from -1 to 1023, as said below
- node_cotangent: bfloat16 [64, 32768], P(None, ('dom', 'sub')), may hold values from -6 to 6
- edge_cotangent: bfloat16 [64, 98304], P(None, ('dom', 'sub')), may hold values from -6 to 6
- edge_first: bfloat16 [192, 64], replicated, may hold values from -0.4375 to 0.4375
- edge_bias: float32 [64], replicated, may hold values from -3 to 3
- edge_second: bfloat16 [64, 64], replicated, may hold values from -0.75 to 0.75
- edge_gain: float32 [64], replicated, may hold values from 0.1 to 1.9
- edge_shift: float32 [64], replicated, may hold values from -3 to 3
- node_first: bfloat16 [128, 64], replicated, may hold values from -0.5 to 0.5
- node_bias: float32 [64], replicated, may hold values from -3 to 3
- node_second: bfloat16 [64, 64], replicated, may hold values from -0.75 to 0.75
- node_gain: float32 [64], replicated, may hold values from 0.1 to 1.9
Outputs:
- delta_state: bfloat16 [64, 32768], P(None, ('dom', 'sub'))
- delta_edges: bfloat16 [64, 98304], P(None, ('dom', 'sub'))
- delta_edgefirst: float32 [192, 64], replicated
- delta_edgebias: float32 [64], replicated
- delta_edgesecond: float32 [64, 64], replicated
- delta_edgegain: float32 [64], replicated
- delta_edgeshift: float32 [64], replicated
- delta_nodefirst: float32 [128, 64], replicated
- delta_nodebias: float32 [64], replicated
- delta_nodesecond: float32 [64, 64], replicated
- delta_nodegain: float32 [64], replicated
- delta_nodeshift: float32 [64], replicated
Inputs may be any that keep to these rules, and one draw needn't show every extreme that they name: `send_index`: block k = o * 4 + t of partition p = d * 4 + s lists own cells that p sends to the partition at dom index d + o - 1 and sub index t: live entries first, then -1. Blocks towards a dom index outside the mesh, and block 4 + s, hold only -1; every other block holds 32 to 128 live entries. Some partition receives a full block from every partition that sends to it. `senders`: an entry below 1024 is an own cell. An entry 1024 + k * 128 + j with k = o * 4 + u names ghost slot j of block k: the j-th entry of block o * 4 + s of the partition at dom index d + 1 - o and sub index u, and that entry is live.
All inputs are finite; a program needn't handle non-finite values.
Results may differ from a plain program's by a relative error of at most 0.0095.
Values may be sent and summed in bfloat16 or wider, within the bound.
A program may use at most 64 MiB of HBM per device.

v0:
```python
import math
import jax
import jax.numpy as jnp
from jax import lax
from jax.sharding import PartitionSpec as P

EPSILON = 1e-05


def from_behind(value, axis, steps):
    count = lax.axis_size(axis)
    first, last = (max(0, -steps), min(count, count - steps))
    return lax.ppermute(value, axis, [(source, source + steps) for source in range(first, last)])


def contract_first(first_operand, second_operand):
    return lax.dot_general(
        first_operand, second_operand, (((0,), (0,)), ((), ())), preferred_element_type=jnp.float32
    )


def contract_last(first_operand, second_operand):
    return lax.dot_general(
        first_operand, second_operand, (((1,), (1,)), ((), ())), preferred_element_type=jnp.float32
    )


def sigmoid_linear(values):
    return values * jax.nn.sigmoid(values)


def sigmoid_slope(values):
    logistic = jax.nn.sigmoid(values)
    return logistic * (1.0 + values * (1.0 - logistic))


def standardize(values):
    centered = values - jnp.mean(values, axis=0, keepdims=True)
    spread = lax.rsqrt(jnp.mean(centered * centered, axis=0, keepdims=True) + EPSILON)
    return (centered * spread, spread)


def normalize_back(upstream, scaled, spread, gain_vector):
    gain_delta = jnp.sum(upstream * scaled, axis=1)
    shift_delta = jnp.sum(upstream, axis=1)
    weighted = upstream * gain_vector[:, None]
    result = spread * (
        weighted
        - jnp.mean(weighted, axis=0, keepdims=True)
        - scaled * jnp.mean(weighted * scaled, axis=0, keepdims=True)
    )
    return (result, gain_delta, shift_delta)


def block_sizes(count, width):
    step = math.gcd(count, 512)
    piece = math.gcd(width, 2048)
    return (step, piece)


def pick_precision(values):
    if values.dtype == jnp.float32:
        return lax.Precision.HIGHEST
    return None


def column_gather(table, index):
    rows, width = table.shape
    count = index.shape[0]
    step, piece = block_sizes(count, width)
    blocks = index.reshape(count // step, step)
    precision = pick_precision(table)

    def one_block(number, result):
        chosen = lax.dynamic_index_in_dim(blocks, number, 0, keepdims=False)
        total = jnp.zeros((rows, step), jnp.float32)
        for begin in range(0, width, piece):
            columns = lax.iota(jnp.int32, piece) + begin
            selector = (columns[:, None] == chosen[None, :]).astype(table.dtype)
            total = total + jnp.dot(
                table[:, begin : begin + piece],
                selector,
                precision=precision,
                preferred_element_type=jnp.float32,
            )
        return lax.dynamic_update_slice_in_dim(result, total.astype(table.dtype), number * step, 1)

    return lax.fori_loop(0, count // step, one_block, jnp.zeros((rows, count), table.dtype))


def column_scatter(values, index, width):
    rows, count = values.shape
    step, piece = block_sizes(count, width)
    blocks = index.reshape(count // step, step)
    precision = pick_precision(values)

    def one_block(number, result):
        chosen = lax.dynamic_index_in_dim(blocks, number, 0, keepdims=False)
        portion = lax.dynamic_slice_in_dim(values, number * step, step, 1)
        pieces = []
        for begin in range(0, width, piece):
            columns = lax.iota(jnp.int32, piece) + begin
            selector = (chosen[:, None] == columns[None, :]).astype(values.dtype)
            pieces.append(
                jnp.dot(portion, selector, precision=precision, preferred_element_type=jnp.float32)
            )
        return result + jnp.concatenate(pieces, axis=1)

    return lax.fori_loop(0, count // step, one_block, jnp.zeros((rows, width), jnp.float32))


def local_backward(
    extended,
    node_state,
    edge_state,
    senders,
    receivers,
    node_cotangent,
    edge_cotangent,
    edge_first,
    edge_bias,
    edge_second,
    edge_gain,
    edge_shift,
    node_first,
    node_bias,
    node_second,
    node_gain,
):
    features, cell_count = node_state.shape
    sender_rows = column_gather(extended, senders)
    receiver_rows = column_gather(node_state, receivers)
    stacked = jnp.concatenate([sender_rows, receiver_rows, edge_state], axis=0)
    edge_linear = contract_first(edge_first, stacked) + edge_bias[:, None]
    edge_active = sigmoid_linear(edge_linear).astype(jnp.bfloat16)
    edge_output = contract_first(edge_second, edge_active)
    edge_scaled, edge_spread = standardize(edge_output)
    message = (edge_scaled * edge_gain[:, None] + edge_shift[:, None]).astype(jnp.bfloat16)
    summed = column_scatter(message, receivers, cell_count)
    node_input = jnp.concatenate([node_state, summed.astype(jnp.bfloat16)], axis=0)
    node_linear = contract_first(node_first, node_input) + node_bias[:, None]
    node_active = sigmoid_linear(node_linear).astype(jnp.bfloat16)
    node_output = contract_first(node_second, node_active)
    node_scaled, node_spread = standardize(node_output)
    upstream = node_cotangent.astype(jnp.float32)
    node_delta, nodegain_delta, nodeshift_delta = normalize_back(
        upstream, node_scaled, node_spread, node_gain
    )
    node_delta = node_delta.astype(jnp.bfloat16)
    nodesecond_delta = contract_last(node_active, node_delta)
    node_hidden = jnp.dot(
        node_second, node_delta, preferred_element_type=jnp.float32
    ) * sigmoid_slope(node_linear)
    nodebias_delta = jnp.sum(node_hidden, axis=1)
    node_hidden = node_hidden.astype(jnp.bfloat16)
    nodefirst_delta = contract_last(node_input, node_hidden)
    node_back = jnp.dot(node_first, node_hidden, preferred_element_type=jnp.float32)
    message_delta = edge_cotangent.astype(jnp.float32) + column_gather(
        node_back[features:], receivers
    )
    edge_delta, edgegain_delta, edgeshift_delta = normalize_back(
        message_delta, edge_scaled, edge_spread, edge_gain
    )
    edge_delta = edge_delta.astype(jnp.bfloat16)
    edgesecond_delta = contract_last(edge_active, edge_delta)
    edge_hidden = jnp.dot(
        edge_second, edge_delta, preferred_element_type=jnp.float32
    ) * sigmoid_slope(edge_linear)
    edgebias_delta = jnp.sum(edge_hidden, axis=1)
    edge_hidden = edge_hidden.astype(jnp.bfloat16)
    edgefirst_delta = contract_last(stacked, edge_hidden)
    edge_back = jnp.dot(edge_first, edge_hidden, preferred_element_type=jnp.float32)
    edge_result = (edge_cotangent.astype(jnp.float32) + edge_back[2 * features :]).astype(
        jnp.bfloat16
    )
    scattered = column_scatter(edge_back[:features], senders, extended.shape[1])
    local_delta = (
        scattered[:, :cell_count]
        + column_scatter(edge_back[features : 2 * features], receivers, cell_count)
        + node_back[:features]
        + upstream
    )
    ghost_delta = scattered[:, cell_count:]
    partials = (
        edgefirst_delta,
        edgebias_delta,
        edgesecond_delta,
        edgegain_delta,
        edgeshift_delta,
        nodefirst_delta,
        nodebias_delta,
        nodesecond_delta,
        nodegain_delta,
        nodeshift_delta,
    )
    return (local_delta, ghost_delta, edge_result, partials)


def on_device(
    node_state,
    edge_state,
    senders,
    receivers,
    send_index,
    node_cotangent,
    edge_cotangent,
    edge_first,
    edge_bias,
    edge_second,
    edge_gain,
    edge_shift,
    node_first,
    node_bias,
    node_second,
    node_gain,
):
    features, cell_count = node_state.shape
    sub_count = lax.axis_size("sub")
    peer_count = 3 * sub_count
    halo_width = send_index.shape[2]
    index_rows = send_index.reshape(peer_count, halo_width)
    live_slots = index_rows >= 0
    safe_index = jnp.where(live_slots, index_rows, 0).reshape(-1)
    picked = column_gather(node_state, safe_index).reshape(features, peer_count, halo_width)
    outgoing = jnp.where(live_slots[None], picked, jnp.zeros_like(picked))
    blocks = outgoing.reshape(features, 3, sub_count, halo_width)
    across = lax.all_to_all(blocks, "sub", split_axis=2, concat_axis=2, tiled=True)
    upper = from_behind(across[:, 0], "dom", -1)
    lower = from_behind(across[:, 2], "dom", 1)
    ghost_rows = jnp.stack([upper, across[:, 1], lower], axis=1).reshape(
        features, peer_count, halo_width
    )
    extended = jnp.concatenate([node_state, ghost_rows.reshape(features, -1)], axis=1)
    local_delta, ghost_delta, edge_result, partials = local_backward(
        extended,
        node_state,
        edge_state,
        senders,
        receivers,
        node_cotangent,
        edge_cotangent,
        edge_first,
        edge_bias,
        edge_second,
        edge_gain,
        edge_shift,
        node_first,
        node_bias,
        node_second,
        node_gain,
    )
    ghost_delta = ghost_delta.reshape(features, peer_count, halo_width)
    grouped = ghost_delta.reshape(features, 3, sub_count, halo_width)
    further = from_behind(grouped[:, 0].astype(jnp.bfloat16), "dom", 1).astype(jnp.float32)
    nearer = from_behind(grouped[:, 2].astype(jnp.bfloat16), "dom", -1).astype(jnp.float32)
    regrouped = jnp.stack([further, grouped[:, 1], nearer], axis=1)
    returned = (
        lax.all_to_all(
            regrouped.astype(jnp.bfloat16), "sub", split_axis=2, concat_axis=2, tiled=True
        )
        .astype(regrouped.dtype)
        .reshape(features, peer_count, halo_width)
    )
    masked = jnp.where(live_slots[None], returned, jnp.zeros_like(returned)).reshape(features, -1)
    local_delta = local_delta + column_scatter(masked, safe_index, cell_count)
    totals = lax.psum(
        (
            partials[0],
            partials[1],
            partials[2],
            partials[3],
            partials[4],
            partials[5],
            partials[6],
            partials[7],
            partials[8],
            partials[9],
        ),
        ("dom", "sub"),
    )
    faces_total = edge_state.shape[1] * lax.axis_size("dom") * sub_count
    factor = 1.0 / math.sqrt(faces_total)
    (
        edgefirst_sum,
        edgebias_sum,
        edgesecond_sum,
        edgegain_sum,
        edgeshift_sum,
        nodefirst_sum,
        nodebias_sum,
        nodesecond_sum,
        nodegain_sum,
        nodeshift_sum,
    ) = totals
    return (
        local_delta.astype(jnp.bfloat16),
        edge_result,
        edgefirst_sum * factor,
        edgebias_sum * factor,
        edgesecond_sum * factor,
        edgegain_sum * factor,
        edgeshift_sum * factor,
        nodefirst_sum * factor,
        nodebias_sum * factor,
        nodesecond_sum * factor,
        nodegain_sum * factor,
        nodeshift_sum * factor,
    )


def solution(mesh):
    in_specs = (
        P(None, ("dom", "sub")),
        P(None, ("dom", "sub")),
        P(("dom", "sub")),
        P(("dom", "sub")),
        P(("dom", "sub"), None, None),
        P(None, ("dom", "sub")),
        P(None, ("dom", "sub")),
        P(),
        P(),
        P(),
        P(),
        P(),
        P(),
        P(),
        P(),
        P(),
    )
    out_specs = (
        P(None, ("dom", "sub")),
        P(None, ("dom", "sub")),
        P(),
        P(),
        P(),
        P(),
        P(),
        P(),
        P(),
        P(),
        P(),
        P(),
    )
    return jax.shard_map(
        on_device, mesh=mesh, in_specs=in_specs, out_specs=out_specs, check_vma=False
    )
```

profile of v0, /device:TPU:8, one launch (start us, length us, event | category | flops | bytes accessed | tf_op | source)
XLA Modules:
  0.0 289.5 jit_solution(8450819076300327334)
XLA Ops:
  8.7 4.2 %while.108 = (s32[]{:T(128)}, bf16[64,1536]{1,0:T(8,128)(2,1)S(1)}, s32[3,512]{1,0:T(4,128)S(1)}, bf16[64,1024]{1,0:T(8,128)(2,1)}, s32[]{:T(128)}, /*index=5*/s32[]{:T(128)}, s32[]{:T(128)}, s32[]{:T(128)}) while((s32[]{:T(128)}, bf16[64,1536]{1,0:T(8,128)(2,1)S(1)}, s32[3,512]{1,0:T(4,128)S(1)}, bf16[64,1024]{1,0:T(8,128)(2,1)}, s32[]{:T(128)}, ...), condition=%wide.region_1.2_spmd, body=%wide.region_0.1_spmd.sunk | while | flops 67665928 | bytes 202891 | solution.py:88
  13.8 3.4 %all-to-all-start = ((bf16[64,3,4,128]{3,0,1,2:T(8,128)(2,1)}), bf16[64,3,4,128]{3,0,1,2:T(8,128)(2,1)S(1)}, u32[]{:S(2)}, u32[]{:S(2)}) async-start(bf16[64,3,4,128]{3,0,1,2:T(8,128)(2,1)} %copy.47), calls=%async_computation | async-start | bytes 393216 | tf_op jit(solution)/shard_map/all_to_all | solution.py:227
  17.3 5.2 %all-to-all-done = bf16[64,3,4,128]{3,0,1,2:T(8,128)(2,1)S(1)} async-done(((bf16[64,3,4,128]{3,0,1,2:T(8,128)(2,1)}), bf16[64,3,4,128]{3,0,1,2:T(8,128)(2,1)S(1)}, u32[]{:S(2)}, u32[]{:S(2)}) %all-to-all-start) | async-done | bytes 196640 | tf_op jit(solution)/shard_map/all_to_all | solution.py:227
  22.5 3.4 %collective-permute-start.1 = (bf16[64,4,128]{2,0,1:T(8,128)(2,1)S(1)}, bf16[64,4,128]{2,0,1:T(8,128)(2,1)S(1)}, u32[]{:S(2)}, u32[]{:S(2)}) collective-permute-start(bf16[64,4,128]{2,0,1:T(8,128)(2,1)S(1)} %get-tuple-element.818), channel_id=1, source_target_pairs={{0,4},{4,8},{8,12},{12,16},{16,20},{20,24},{24,28},{1,5},{5,9},{9,... | collective-permute-start | bytes 196616 | tf_op jit(solution)/shard_map/ppermute | solution.py:13
  25.9 3.3 %collective-permute-start = (bf16[64,4,128]{2,0,1:T(8,128)(2,1)S(1)}, bf16[64,4,128]{2,0,1:T(8,128)(2,1)S(1)}, u32[]{:S(2)}, u32[]{:S(2)}) collective-permute-start(bf16[64,4,128]{2,0,1:T(8,128)(2,1)S(1)} %get-tuple-element.817), channel_id=1, source_target_pairs={{4,0},{8,4},{12,8},{16,12},{20,16},{24,20},{28,24},{5,1},{9,5},{13... | collective-permute-start | bytes 196616 | tf_op jit(solution)/shard_map/ppermute | solution.py:13
  29.3 3.0 %while.110 = (s32[]{:T(128)}, bf16[64,3072]{1,0:T(8,128)(2,1)S(1)}, s32[6,512]{1,0:T(8,128)S(1)}, bf16[64,1024]{1,0:T(8,128)(2,1)S(1)}, s32[]{:T(128)}, /*index=5*/s32[]{:T(128)}, s32[]{:T(128)}, s32[]{:T(128)}) while((s32[]{:T(128)}, bf16[64,3072]{1,0:T(8,128)(2,1)S(1)}, s32[6,512]{1,0:T(8,128)S(1)}, bf16[64,1024]{1,0:T(8,128)(2,1)S(1)}, ...), condition=%wide.region_5.6_spmd, body=%wide.region_4.5_spmd.sunk | while | flops 67665928 | bytes 202891 | solution.py:88
  32.8 11.0 %while.109 = (s32[]{:T(128)}, bf16[64,3072]{1,0:T(8,128)(2,1)S(1)}, s32[6,512]{1,0:T(8,128)S(1)}, bf16[64,1024]{1,0:T(8,128)(2,1)S(1)}, bf16[64,1536]{1,0:T(8,12...) while((s32[]{:T(128)}, bf16[64,3072]{1,0:T(8,128)(2,1)S(1)}, s32[6,512]{1,0:T(8,128)S(1)}, ...), condition=%wide.region_3.4_spmd, body=%wide.region_2.3_spmd.sunk | while | flops 169248768 | bytes 1472659 | solution.py:88
  47.2 3.7 %while.112 = (s32[]{:T(128)}, f32[64,1024]{1,0:T(8,128)S(1)}, bf16[64,3072]{1,0:T(8,128)(2,1)S(1)}, s32[6,512]{1,0:T(8,128)S(1)}, s32[]{:T(128)}, /*index=5*/s32[]{:T(128)}, s32[]{:T(128)}, s32[]{:T(128)}) while((s32[]{:T(128)}, f32[64,1024]{1,0:T(8,128)S(1)}, bf16[64,3072]{1,0:T(8,128)(2,1)S(1)}, s32[6,512]{1,0:T(8,128)S(1)}, ...), condition=%wide.region_9.10_spmd.clone, body=%wide.region_8.9_spmd.clone.sunk | while | flops 67764232 | bytes 596117 | solution.py:109
  56.0 11.1 %while.111 = (s32[]{:T(128)}, f32[64,3072]{1,0:T(8,128)S(1)}, s32[6,512]{1,0:T(8,128)S(1)}, f32[64,1024]{1,0:T(8,128)}, s32[]{:T(128)}, /*index=5*/s32[]{:T(128)}, s32[]{:T(128)}, s32[]{:T(128)}) while((s32[]{:T(128)}, f32[64,3072]{1,0:T(8,128)S(1)}, s32[6,512]{1,0:T(8,128)S(1)}, f32[64,1024]{1,0:T(8,128)}, s32[]{:T(128)}, ...), condition=%wide.region_15.16_spmd, body=%wide.region_14.15_spmd.sunk | while | flops 403177472 | bytes 399499 | solution.py:88
  56.1 1.8 fusion.184
  58.0 1.8 fusion.184
  59.8 1.8 fusion.184
  61.7 1.8 fusion.184
  63.5 1.8 fusion.184
  65.4 1.8 fusion.184
  73.9 45.6 %while.113 = (s32[]{:T(128)}, f32[64,2560]{1,0:T(8,128)S(1)}, f32[64,3072]{1,0:T(8,128)}, s32[6,512]{1,0:T(8,128)S(1)}, s32[]{:T(128)}, /*index=5*/s32[]{:T(128)}, s32[]{:T(128)}, s32[]{:T(128)}) while((s32[]{:T(128)}, f32[64,2560]{1,0:T(8,128)S(1)}, f32[64,3072]{1,0:T(8,128)}, s32[6,512]{1,0:T(8,128)S(1)}, s32[]{:T(128)}, ...), condition=%wide.region_19.20_spmd.clone, body=%wide.region_18.19_spmd.clone.sunk | while | flops 1008273408 | bytes 3307685 | solution.py:109
  73.9 1.5 convolution_dynamic-update-slice_fusion.10
  119.7 4.0 %collective-permute-start.2 = (bf16[64,4,128]{2,1,0:T(4,128)(2,1)S(1)}, bf16[64,4,128]{2,1,0:T(4,128)(2,1)S(1)}, u32[]{:S(2)}, u32[]{:S(2)}) collective-permute-start(bf16[64,4,128]{2,1,0:T(4,128)(2,1)S(1)} %get-tuple-element.814), channel_id=1, source_target_pairs={{0,4},{4,8},{8,12},{12,16},{16,20},{20,24},{24,28},{1,5},{5,9},{9,... | collective-permute-start | bytes 196616 | tf_op jit(solution)/shard_map/ppermute | solution.py:13
  123.6 2.9 %collective-permute-start.3 = (bf16[64,4,128]{2,1,0:T(4,128)(2,1)S(1)}, bf16[64,4,128]{2,1,0:T(4,128)(2,1)S(1)}, u32[]{:S(2)}, u32[]{:S(2)}) collective-permute-start(bf16[64,4,128]{2,1,0:T(4,128)(2,1)S(1)} %get-tuple-element.815), channel_id=1, source_target_pairs={{4,0},{8,4},{12,8},{16,12},{20,16},{24,20},{28,24},{5,1},{9,5},{13... | collective-permute-start | bytes 196616 | tf_op jit(solution)/shard_map/ppermute | solution.py:13
  126.6 6.2 %while.114 = (s32[]{:T(128)}, f32[64,1024]{1,0:T(8,128)S(1)}, f32[64,3072]{1,0:T(8,128)S(1)}, s32[6,512]{1,0:T(8,128)S(1)}, s32[]{:T(128)}, /*index=5*/s32[]{:T(128)}, s32[]{:T(128)}, s32[]{:T(128)}) while((s32[]{:T(128)}, f32[64,1024]{1,0:T(8,128)S(1)}, f32[64,3072]{1,0:T(8,128)S(1)}, s32[6,512]{1,0:T(8,128)S(1)}, s32[]{:T(128)}, ...), condition=%wide.region_21.22_spmd.clone, body=%wide.region_20.21_spmd.clone.sunk | while | flops 403308544 | bytes 661653 | solution.py:109
  132.9 124.7 %all-reduce.3.cloned.1.call-done = (f32[192,64]{0,1:T(8,128)}, f32[64]{0:T(128)}, f32[64,64]{1,0:T(8,128)}, f32[64]{0:T(128)}, f32[64]{0:T(128)}, /*index=5*/f32...) async-done(((f32[192,64]{0,1:T(8,128)}, f32[64]{0:T(128)}, f32[64,64]{1,0:T(8,128)}, f32[64]{0:T(128)}, f32[64]{0:T(128)}, ...) | async-done | bytes 116240 | tf_op jit(solution)/shard_map/psum | solution.py:266
  269.8 3.4 %all-to-all-start.1 = ((bf16[64,3,4,128]{3,0,1,2:T(8,128)(2,1)}), bf16[64,3,4,128]{3,0,1,2:T(8,128)(2,1)S(1)}, u32[]{:S(2)}, u32[]{:S(2)}) async-start(bf16[64,3,4,128]{3,0,1,2:T(8,128)(2,1)} %copy.54), calls=%async_computation.1 | async-start | bytes 393216 | tf_op jit(solution)/shard_map/all_to_all | solution.py:258
  274.3 4.1 %all-to-all-done.1 = bf16[64,3,4,128]{3,0,1,2:T(8,128)(2,1)S(1)} async-done(((bf16[64,3,4,128]{3,0,1,2:T(8,128)(2,1)}), bf16[64,3,4,128]{3,0,1,2:T(8,128)(2,1)S(1)}, u32[]{:S(2)}, u32[]{:S(2)}) %all-to-all-start.1) | async-done | bytes 196640 | tf_op jit(solution)/shard_map/all_to_all | solution.py:258
  278.8 3.1 %while.115 = (s32[]{:T(128)}, f32[64,1024]{1,0:T(8,128)S(1)}, f32[64,1536]{1,0:T(8,128)S(1)}, s32[3,512]{1,0:T(4,128)S(1)}, s32[]{:T(128)}, /*index=5*/s32[]{:T(128)}, s32[]{:T(128)}, s32[]{:T(128)}) while((s32[]{:T(128)}, f32[64,1024]{1,0:T(8,128)S(1)}, f32[64,1536]{1,0:T(8,128)S(1)}, s32[3,512]{1,0:T(4,128)S(1)}, s32[]{:T(128)}, ...), condition=%wide.region_23.24_spmd.clone, body=%wide.region_22.23_spmd.clone.sunk | while | flops 403308544 | bytes 661653 | solution.py:109
  (302 shorter events, 106.0 us)
Async XLA Ops:
  7.2 36.8 %copy-start = (bf16[192,64]{0,1:T(8,128)(2,1)S(1)}, bf16[192,64]{0,1:T(8,128)(2,1)}, u32[]{:S(2)}) copy-start(bf16[192,64]{0,1:T(8,128)(2,1)} %param.39) | copy-start | bytes 73732
  8.7 8.6 %copy-start.13 = (s32[3072]{0:T(1024)S(1)}, s32[3072]{0:T(1024)}, u32[]{:S(2)}) copy-start(s32[3072]{0:T(1024)} %param.35) | copy-start | bytes 36868
  12.9 16.3 %copy-start.18 = (bf16[64,1024]{1,0:T(8,128)(2,1)S(1)}, bf16[64,1024]{1,0:T(8,128)(2,1)}, u32[]{:S(2)}) copy-start(bf16[64,1024]{1,0:T(8,128)(2,1)} %get-tuple-element.1290) | copy-start | bytes 393220
  13.8 8.6 %all-to-all-start = ((bf16[64,3,4,128]{3,0,1,2:T(8,128)(2,1)}), bf16[64,3,4,128]{3,0,1,2:T(8,128)(2,1)S(1)}, u32[]{:S(2)}, u32[]{:S(2)}) async-start(bf16[64,3,4,128]{3,0,1,2:T(8,128)(2,1)} %copy.47), calls=%async_computation | async-start | bytes 393216 | tf_op jit(solution)/shard_map/all_to_all | solution.py:227
  17.2 240.4 %all-reduce.3.cloned.1.call-start = ((), (), s32[]{:S(2)}) async-start(), calls=%async_computation.2 | async-start | bytes 333824 | tf_op jit(solution)/shard_map/psum | solution.py:266
  22.5 9.9 %collective-permute-start.1 = (bf16[64,4,128]{2,0,1:T(8,128)(2,1)S(1)}, bf16[64,4,128]{2,0,1:T(8,128)(2,1)S(1)}, u32[]{:S(2)}, u32[]{:S(2)}) collective-permute-start(bf16[64,4,128]{2,0,1:T(8,128)(2,1)S(1)} %get-tuple-element.818), channel_id=1, source_target_pairs={{0,4},{4,8},{8,12},{12,16},{16,20},{20,24},{24,28},{1,5},{5,9},{9,... | collective-permute-start | bytes 196616 | tf_op jit(solution)/shard_map/ppermute | solution.py:13
  25.9 6.5 %collective-permute-start = (bf16[64,4,128]{2,0,1:T(8,128)(2,1)S(1)}, bf16[64,4,128]{2,0,1:T(8,128)(2,1)S(1)}, u32[]{:S(2)}, u32[]{:S(2)}) collective-permute-start(bf16[64,4,128]{2,0,1:T(8,128)(2,1)S(1)} %get-tuple-element.817), channel_id=1, source_target_pairs={{4,0},{8,4},{12,8},{16,12},{20,16},{24,20},{28,24},{5,1},{9,5},{13... | collective-permute-start | bytes 196616 | tf_op jit(solution)/shard_map/ppermute | solution.py:13
  29.3 3.1 %copy-start.14 = (s32[3072]{0:T(1024)S(1)}, s32[3072]{0:T(1024)}, u32[]{:S(2)}) copy-start(s32[3072]{0:T(1024)} %param.34) | copy-start | bytes 36868
  32.8 11.1 %copy-start.7 = (bf16[64,3072]{1,0:T(8,128)(2,1)S(1)}, bf16[64,3072]{1,0:T(8,128)(2,1)}, u32[]{:S(2)}) copy-start(bf16[64,3072]{1,0:T(8,128)(2,1)} %param.33) | copy-start | bytes 1179652
  44.5 1.3 copy-start.2
  44.5 2.0 copy-start.10
  44.5 2.5 copy-start.15
  44.5 2.5 copy-start.17
  47.2 3.8 %copy-start.12 = (bf16[128,64]{0,1:T(8,128)(2,1)S(1)}, bf16[128,64]{0,1:T(8,128)(2,1)}, u32[]{:S(2)}) copy-start(bf16[128,64]{0,1:T(8,128)(2,1)} %param.44) | copy-start | bytes 49156
  47.2 3.8 %copy-start.20 = (f32[64]{0:T(128)S(1)}, f32[64]{0:T(128)}, u32[]{:S(2)}) copy-start(f32[64]{0:T(128)} %param.45) | copy-start | bytes 772
  47.2 4.0 %copy-start.11 = (bf16[64,64]{1,0:T(8,128)(2,1)S(1)}, bf16[64,64]{1,0:T(8,128)(2,1)}, u32[]{:S(2)}) copy-start(bf16[64,64]{1,0:T(8,128)(2,1)} %param.46) | copy-start | bytes 24580
  56.0 11.2 %copy-start.1 = (bf16[64,3072]{1,0:T(8,128)(2,1)S(1)}, bf16[64,3072]{1,0:T(8,128)(2,1)}, u32[]{:S(2)}) copy-start(bf16[64,3072]{1,0:T(8,128)(2,1)} %param.38) | copy-start | bytes 1179652
  67.2 1.7 copy-start.5
  69.7 1.3 copy-start.3
  73.8 52.8 %copy-start.9 = (f32[64,1024]{1,0:T(8,128)S(1)}, f32[64,1024]{1,0:T(8,128)}, u32[]{:S(2)}) copy-start(f32[64,1024]{1,0:T(8,128)} %custom-call.2) | copy-start | bytes 786436
  119.7 149.3 %collective-permute-start.2 = (bf16[64,4,128]{2,1,0:T(4,128)(2,1)S(1)}, bf16[64,4,128]{2,1,0:T(4,128)(2,1)S(1)}, u32[]{:S(2)}, u32[]{:S(2)}) collective-permute-start(bf16[64,4,128]{2,1,0:T(4,128)(2,1)S(1)} %get-tuple-element.814), channel_id=1, source_target_pairs={{0,4},{4,8},{8,12},{12,16},{16,20},{20,24},{24,28},{1,5},{5,9},{9,... | collective-permute-start | bytes 196616 | tf_op jit(solution)/shard_map/ppermute | solution.py:13
  123.6 145.3 %collective-permute-start.3 = (bf16[64,4,128]{2,1,0:T(4,128)(2,1)S(1)}, bf16[64,4,128]{2,1,0:T(4,128)(2,1)S(1)}, u32[]{:S(2)}, u32[]{:S(2)}) collective-permute-start(bf16[64,4,128]{2,1,0:T(4,128)(2,1)S(1)} %get-tuple-element.815), channel_id=1, source_target_pairs={{4,0},{8,4},{12,8},{16,12},{20,16},{24,20},{28,24},{5,1},{9,5},{13... | collective-permute-start | bytes 196616 | tf_op jit(solution)/shard_map/ppermute | solution.py:13
  132.9 145.9 %copy-start.8 = (f32[64,1024]{1,0:T(8,128)S(1)}, f32[64,1024]{1,0:T(8,128)}, u32[]{:S(2)}) copy-start(f32[64,1024]{1,0:T(8,128)} %custom-call.3) | copy-start | bytes 786436
  269.8 8.6 %all-to-all-start.1 = ((bf16[64,3,4,128]{3,0,1,2:T(8,128)(2,1)}), bf16[64,3,4,128]{3,0,1,2:T(8,128)(2,1)S(1)}, u32[]{:S(2)}, u32[]{:S(2)}) async-start(bf16[64,3,4,128]{3,0,1,2:T(8,128)(2,1)} %copy.54), calls=%async_computation.1 | async-start | bytes 393216 | tf_op jit(solution)/shard_map/all_to_all | solution.py:258
  (5 other events, 4.4 us)
Sparse Core Ops, SparseCore 0:
  126.7 130.8 all-reduce.2
where the time goes:
time: 291 us; the launch traced here: 289 us
  waiting for transfers between devices  134 us (46%)
  matrix products  92.7 us (32%)
  starting transfers between devices  20.4 us (7%)
  other arithmetic  20.3 us (7%)
  between operations  14.7 us (5%)
  local copies, waits for them, and re-layouts  5.33 us (2%)
    psum x1, waiting for transfers between devices, on_device(): lax.psum((partials[0], partials[1], partials[2], partials[3], partials[4]...  125 us
    dot_general x45, matrix products, one_block(): jnp.dot(portion, selector, precision=precision, preferred_element_type=jn...  56.2 us
    dot_general x45, matrix products, one_block(): jnp.dot(table[:, begin:begin + piece], selector, precision=precision, pre...  28.1 us
    ppermute x4, starting transfers between devices, from_behind(): lax.ppermute(value, axis, [(source, source + steps) for source in range(f...  13.7 us
  transfers between devices with their start and end apart: 7, of which 3 were waited for; matrix products, arithmetic and copies ran while one was open for 7% of the time, Pallas kernels for 0%

commit v1 on v0

--- a/solution.py
+++ b/solution.py
@@ -264,19 +264,22 @@
     masked = jnp.where(live_slots[None], returned, jnp.zeros_like(returned)).reshape(features, -1)
     local_delta = local_delta + column_scatter(masked, safe_index, cell_count)
     totals = lax.psum(
-        (
-            partials[0],
-            partials[1],
-            partials[2],
-            partials[3],
-            partials[4],
-            partials[5],
-            partials[6],
-            partials[7],
-            partials[8],
-            partials[9],
+        lax.psum(
+            (
+                partials[0],
+                partials[1],
+                partials[2],
+                partials[3],
+                partials[4],
+                partials[5],
+                partials[6],
+                partials[7],
+                partials[8],
+                partials[9],
+            ),
+            "dom",
         ),
-        ("dom", "sub"),
+        "sub",
     )
     faces_total = edge_state.shape[1] * lax.axis_size("dom") * sub_count
     factor = 1.0 / math.sqrt(faces_total)

time: 291 us -> 260 us (0.89)
  waiting for transfers between devices: 134 us -> 101 us
    psum x1, waiting for transfers between devices: 125 us -> 65.9 us  [on_device(): lax.psum((partials[0], partials[1], partials[2], partials[3], partials[4]...]
    psum x0 -> x1, waiting for transfers between devices: none -> 30.3 us  [on_device(): lax.psum(lax.psum((partials[0], partials[1], partials[2], partials[3], pa...]
    all_to_all x1, waiting for transfers between devices: 4.15 us -> 0.01 us  [on_device(): lax.all_to_all(regrouped.astype(jnp.bfloat16), 'sub', split_axis=2, conca...]
  transfers between devices with their start and end apart: 7 -> 8, of which waited for: 3 -> 3; matrix products, arithmetic and copies ran while one was open for 7% -> 9% of each run, Pallas kernels for 0% -> 0%
where the time goes in v1:
time: 260 us; the launch traced here: 257 us
  waiting for transfers between devices  101 us (39%)
  matrix products  92.7 us (36%)
  starting transfers between devices  20.5 us (8%)
  other arithmetic  20.2 us (8%)
  between operations  14.7 us (6%)
  local copies, waits for them, and re-layouts  5.32 us (2%)
    psum x1, waiting for transfers between devices, on_device(): lax.psum((partials[0], partials[1], partials[2], partials[3], partials[4]...  65.9 us
    dot_general x45, matrix products, one_block(): jnp.dot(portion, selector, precision=precision, preferred_element_type=jn...  56.2 us
    psum x1, waiting for transfers between devices, on_device(): lax.psum(lax.psum((partials[0], partials[1], partials[2], partials[3], pa...  30.3 us
    dot_general x45, matrix products, one_block(): jnp.dot(table[:, begin:begin + piece], selector, precision=precision, pre...  28.1 us
    ppermute x4, starting transfers between devices, from_behind(): lax.ppermute(value, axis, [(source, source + steps) for source in range(f...  13.5 us
  transfers between devices with their start and end apart: 8, of which 3 were waited for; matrix products, arithmetic and copies ran while one was open for 9% of the time, Pallas kernels for 0%

profile of v1, /device:TPU:8, one launch (start us, length us, event | category | flops | bytes accessed | tf_op | source)
XLA Modules:
  0.0 256.9 jit_solution(16681501918363239823)
XLA Ops:
  8.7 4.2 %while.108 = (s32[]{:T(128)}, bf16[64,1536]{1,0:T(8,128)(2,1)S(1)}, s32[3,512]{1,0:T(4,128)S(1)}, bf16[64,1024]{1,0:T(8,128)(2,1)}, s32[]{:T(128)}, /*index=5*/s32[]{:T(128)}, s32[]{:T(128)}, s32[]{:T(128)}) while((s32[]{:T(128)}, bf16[64,1536]{1,0:T(8,128)(2,1)S(1)}, s32[3,512]{1,0:T(4,128)S(1)}, bf16[64,1024]{1,0:T(8,128)(2,1)}, s32[]{:T(128)}, ...), condition=%wide.region_1.2_spmd, body=%wide.region_0.1_spmd.sunk | while | flops 67665928 | bytes 202891 | solution.py:88
  13.8 3.4 %all-to-all-start = ((bf16[64,3,4,128]{3,0,1,2:T(8,128)(2,1)}), bf16[64,3,4,128]{3,0,1,2:T(8,128)(2,1)S(1)}, u32[]{:S(2)}, u32[]{:S(2)}) async-start(bf16[64,3,4,128]{3,0,1,2:T(8,128)(2,1)} %copy.47), calls=%async_computation | async-start | bytes 393216 | tf_op jit(solution)/shard_map/all_to_all | solution.py:227
  17.3 5.2 %all-to-all-done = bf16[64,3,4,128]{3,0,1,2:T(8,128)(2,1)S(1)} async-done(((bf16[64,3,4,128]{3,0,1,2:T(8,128)(2,1)}), bf16[64,3,4,128]{3,0,1,2:T(8,128)(2,1)S(1)}, u32[]{:S(2)}, u32[]{:S(2)}) %all-to-all-start) | async-done | bytes 196640 | tf_op jit(solution)/shard_map/all_to_all | solution.py:227
  22.5 3.4 %collective-permute-start.1 = (bf16[64,4,128]{2,0,1:T(8,128)(2,1)S(1)}, bf16[64,4,128]{2,0,1:T(8,128)(2,1)S(1)}, u32[]{:S(2)}, u32[]{:S(2)}) collective-permute-start(bf16[64,4,128]{2,0,1:T(8,128)(2,1)S(1)} %get-tuple-element.828), channel_id=1, source_target_pairs={{0,4},{4,8},{8,12},{12,16},{16,20},{20,24},{24,28},{1,5},{5,9},{9,... | collective-permute-start | bytes 196616 | tf_op jit(solution)/shard_map/ppermute | solution.py:13
  25.9 3.3 %collective-permute-start = (bf16[64,4,128]{2,0,1:T(8,128)(2,1)S(1)}, bf16[64,4,128]{2,0,1:T(8,128)(2,1)S(1)}, u32[]{:S(2)}, u32[]{:S(2)}) collective-permute-start(bf16[64,4,128]{2,0,1:T(8,128)(2,1)S(1)} %get-tuple-element.827), channel_id=1, source_target_pairs={{4,0},{8,4},{12,8},{16,12},{20,16},{24,20},{28,24},{5,1},{9,5},{13... | collective-permute-start | bytes 196616 | tf_op jit(solution)/shard_map/ppermute | solution.py:13
  29.3 3.0 %while.110 = (s32[]{:T(128)}, bf16[64,3072]{1,0:T(8,128)(2,1)S(1)}, s32[6,512]{1,0:T(8,128)S(1)}, bf16[64,1024]{1,0:T(8,128)(2,1)S(1)}, s32[]{:T(128)}, /*index=5*/s32[]{:T(128)}, s32[]{:T(128)}, s32[]{:T(128)}) while((s32[]{:T(128)}, bf16[64,3072]{1,0:T(8,128)(2,1)S(1)}, s32[6,512]{1,0:T(8,128)S(1)}, bf16[64,1024]{1,0:T(8,128)(2,1)S(1)}, ...), condition=%wide.region_5.6_spmd, body=%wide.region_4.5_spmd.sunk | while | flops 67665928 | bytes 202891 | solution.py:88
  32.8 11.0 %while.109 = (s32[]{:T(128)}, bf16[64,3072]{1,0:T(8,128)(2,1)S(1)}, s32[6,512]{1,0:T(8,128)S(1)}, bf16[64,1024]{1,0:T(8,128)(2,1)S(1)}, bf16[64,1536]{1,0:T(8,12...) while((s32[]{:T(128)}, bf16[64,3072]{1,0:T(8,128)(2,1)S(1)}, s32[6,512]{1,0:T(8,128)S(1)}, ...), condition=%wide.region_3.4_spmd, body=%wide.region_2.3_spmd.sunk | while | flops 169248768 | bytes 1472659 | solution.py:88
  47.2 3.7 %while.112 = (s32[]{:T(128)}, f32[64,1024]{1,0:T(8,128)S(1)}, bf16[64,3072]{1,0:T(8,128)(2,1)S(1)}, s32[6,512]{1,0:T(8,128)S(1)}, s32[]{:T(128)}, /*index=5*/s32[]{:T(128)}, s32[]{:T(128)}, s32[]{:T(128)}) while((s32[]{:T(128)}, f32[64,1024]{1,0:T(8,128)S(1)}, bf16[64,3072]{1,0:T(8,128)(2,1)S(1)}, s32[6,512]{1,0:T(8,128)S(1)}, ...), condition=%wide.region_9.10_spmd.clone, body=%wide.region_8.9_spmd.clone.sunk | while | flops 67764232 | bytes 596117 | solution.py:109
  56.1 11.1 %while.111 = (s32[]{:T(128)}, f32[64,3072]{1,0:T(8,128)S(1)}, s32[6,512]{1,0:T(8,128)S(1)}, f32[64,1024]{1,0:T(8,128)}, s32[]{:T(128)}, /*index=5*/s32[]{:T(128)}, s32[]{:T(128)}, s32[]{:T(128)}) while((s32[]{:T(128)}, f32[64,3072]{1,0:T(8,128)S(1)}, s32[6,512]{1,0:T(8,128)S(1)}, f32[64,1024]{1,0:T(8,128)}, s32[]{:T(128)}, ...), condition=%wide.region_15.16_spmd, body=%wide.region_14.15_spmd.sunk | while | flops 403177472 | bytes 399499 | solution.py:88
  56.1 1.8 fusion.184
  58.0 1.8 fusion.184
  59.9 1.8 fusion.184
  61.7 1.8 fusion.184
  63.6 1.8 fusion.184
  65.4 1.8 fusion.184
  73.9 45.6 %while.113 = (s32[]{:T(128)}, f32[64,2560]{1,0:T(8,128)S(1)}, f32[64,3072]{1,0:T(8,128)}, s32[6,512]{1,0:T(8,128)S(1)}, s32[]{:T(128)}, /*index=5*/s32[]{:T(128)}, s32[]{:T(128)}, s32[]{:T(128)}) while((s32[]{:T(128)}, f32[64,2560]{1,0:T(8,128)S(1)}, f32[64,3072]{1,0:T(8,128)}, s32[6,512]{1,0:T(8,128)S(1)}, s32[]{:T(128)}, ...), condition=%wide.region_19.20_spmd.clone, body=%wide.region_18.19_spmd.clone.sunk | while | flops 1008273408 | bytes 3307685 | solution.py:109
  73.9 1.5 convolution_dynamic-update-slice_fusion.10
  119.7 4.0 %collective-permute-start.2 = (bf16[64,4,128]{2,1,0:T(4,128)(2,1)S(1)}, bf16[64,4,128]{2,1,0:T(4,128)(2,1)S(1)}, u32[]{:S(2)}, u32[]{:S(2)}) collective-permute-start(bf16[64,4,128]{2,1,0:T(4,128)(2,1)S(1)} %get-tuple-element.824), channel_id=1, source_target_pairs={{0,4},{4,8},{8,12},{12,16},{16,20},{20,24},{24,28},{1,5},{5,9},{9,... | collective-permute-start | bytes 196616 | tf_op jit(solution)/shard_map/ppermute | solution.py:13
  123.7 2.8 %collective-permute-start.3 = (bf16[64,4,128]{2,1,0:T(4,128)(2,1)S(1)}, bf16[64,4,128]{2,1,0:T(4,128)(2,1)S(1)}, u32[]{:S(2)}, u32[]{:S(2)}) collective-permute-start(bf16[64,4,128]{2,1,0:T(4,128)(2,1)S(1)} %get-tuple-element.825), channel_id=1, source_target_pairs={{4,0},{8,4},{12,8},{16,12},{20,16},{24,20},{28,24},{5,1},{9,5},{13... | collective-permute-start | bytes 196616 | tf_op jit(solution)/shard_map/ppermute | solution.py:13
  126.7 6.2 %while.114 = (s32[]{:T(128)}, f32[64,1024]{1,0:T(8,128)S(1)}, f32[64,3072]{1,0:T(8,128)S(1)}, s32[6,512]{1,0:T(8,128)S(1)}, s32[]{:T(128)}, /*index=5*/s32[]{:T(128)}, s32[]{:T(128)}, s32[]{:T(128)}) while((s32[]{:T(128)}, f32[64,1024]{1,0:T(8,128)S(1)}, f32[64,3072]{1,0:T(8,128)S(1)}, s32[6,512]{1,0:T(8,128)S(1)}, s32[]{:T(128)}, ...), condition=%wide.region_21.22_spmd.clone, body=%wide.region_20.21_spmd.clone.sunk | while | flops 403308544 | bytes 661653 | solution.py:109
  133.0 65.9 %all-reduce.5.cloned.1.call-done = (f32[192,64]{0,1:T(8,128)}, f32[64]{0:T(128)}, f32[64,64]{1,0:T(8,128)}, f32[64]{0:T(128)}, f32[64]{0:T(128)}, /*index=5*/f32...) async-done(((f32[192,64]{0,1:T(8,128)}, f32[64]{0:T(128)}, f32[64,64]{1,0:T(8,128)}, f32[64]{0:T(128)}, f32[64]{0:T(128)}, ...) | async-done | bytes 116240 | tf_op jit(solution)/shard_map/psum | solution.py:267
  199.8 3.4 %all-to-all-start.1 = ((bf16[64,3,4,128]{3,0,1,2:T(8,128)(2,1)}), bf16[64,3,4,128]{3,0,1,2:T(8,128)(2,1)S(1)}, u32[]{:S(2)}, u32[]{:S(2)}) async-start(bf16[64,3,4,128]{3,0,1,2:T(8,128)(2,1)} %copy.54), calls=%async_computation.1 | async-start | bytes 393216 | tf_op jit(solution)/shard_map/all_to_all | solution.py:258
  203.2 30.3 %all-reduce.7.cloned.1.call-done = (f32[192,64]{0,1:T(8,128)}, f32[64]{0:T(128)}, f32[64,64]{1,0:T(8,128)}, f32[64]{0:T(128)}, f32[64]{0:T(128)}, /*index=5*/f32...) async-done(((f32[192,64]{0,1:T(8,128)}, f32[64]{0:T(128)}, f32[64,64]{1,0:T(8,128)}, f32[64]{0:T(128)}, f32[64]{0:T(128)}, ...) | async-done | bytes 116240 | tf_op jit(solution)/shard_map/psum | solution.py:266
  246.2 3.1 %while.115 = (s32[]{:T(128)}, f32[64,1024]{1,0:T(8,128)S(1)}, f32[64,1536]{1,0:T(8,128)S(1)}, s32[3,512]{1,0:T(4,128)S(1)}, s32[]{:T(128)}, /*index=5*/s32[]{:T(128)}, s32[]{:T(128)}, s32[]{:T(128)}) while((s32[]{:T(128)}, f32[64,1024]{1,0:T(8,128)S(1)}, f32[64,1536]{1,0:T(8,128)S(1)}, s32[3,512]{1,0:T(4,128)S(1)}, s32[]{:T(128)}, ...), condition=%wide.region_23.24_spmd.clone, body=%wide.region_22.23_spmd.clone.sunk | while | flops 403308544 | bytes 661653 | solution.py:109
  (305 shorter events, 106.2 us)
Async XLA Ops:
  7.2 36.8 %copy-start = (bf16[192,64]{0,1:T(8,128)(2,1)S(1)}, bf16[192,64]{0,1:T(8,128)(2,1)}, u32[]{:S(2)}) copy-start(bf16[192,64]{0,1:T(8,128)(2,1)} %param.39) | copy-start | bytes 73732
  8.7 8.6 %copy-start.13 = (s32[3072]{0:T(1024)S(1)}, s32[3072]{0:T(1024)}, u32[]{:S(2)}) copy-start(s32[3072]{0:T(1024)} %param.35) | copy-start | bytes 36868
  12.9 16.3 %copy-start.18 = (bf16[64,1024]{1,0:T(8,128)(2,1)S(1)}, bf16[64,1024]{1,0:T(8,128)(2,1)}, u32[]{:S(2)}) copy-start(bf16[64,1024]{1,0:T(8,128)(2,1)} %get-tuple-element.1342) | copy-start | bytes 393220
  13.8 8.6 %all-to-all-start = ((bf16[64,3,4,128]{3,0,1,2:T(8,128)(2,1)}), bf16[64,3,4,128]{3,0,1,2:T(8,128)(2,1)S(1)}, u32[]{:S(2)}, u32[]{:S(2)}) async-start(bf16[64,3,4,128]{3,0,1,2:T(8,128)(2,1)} %copy.47), calls=%async_computation | async-start | bytes 393216 | tf_op jit(solution)/shard_map/all_to_all | solution.py:227
  17.2 181.7 %all-reduce.5.cloned.1.call-start = ((), (), s32[]{:S(2)}) async-start(), calls=%async_computation.2 | async-start | bytes 333824 | tf_op jit(solution)/shard_map/psum | solution.py:267
  22.5 9.9 %collective-permute-start.1 = (bf16[64,4,128]{2,0,1:T(8,128)(2,1)S(1)}, bf16[64,4,128]{2,0,1:T(8,128)(2,1)S(1)}, u32[]{:S(2)}, u32[]{:S(2)}) collective-permute-start(bf16[64,4,128]{2,0,1:T(8,128)(2,1)S(1)} %get-tuple-element.828), channel_id=1, source_target_pairs={{0,4},{4,8},{8,12},{12,16},{16,20},{20,24},{24,28},{1,5},{5,9},{9,... | collective-permute-start | bytes 196616 | tf_op jit(solution)/shard_map/ppermute | solution.py:13
  25.9 6.5 %collective-permute-start = (bf16[64,4,128]{2,0,1:T(8,128)(2,1)S(1)}, bf16[64,4,128]{2,0,1:T(8,128)(2,1)S(1)}, u32[]{:S(2)}, u32[]{:S(2)}) collective-permute-start(bf16[64,4,128]{2,0,1:T(8,128)(2,1)S(1)} %get-tuple-element.827), channel_id=1, source_target_pairs={{4,0},{8,4},{12,8},{16,12},{20,16},{24,20},{28,24},{5,1},{9,5},{13... | collective-permute-start | bytes 196616 | tf_op jit(solution)/shard_map/ppermute | solution.py:13
  29.3 3.1 %copy-start.14 = (s32[3072]{0:T(1024)S(1)}, s32[3072]{0:T(1024)}, u32[]{:S(2)}) copy-start(s32[3072]{0:T(1024)} %param.34) | copy-start | bytes 36868
  32.8 11.1 %copy-start.7 = (bf16[64,3072]{1,0:T(8,128)(2,1)S(1)}, bf16[64,3072]{1,0:T(8,128)(2,1)}, u32[]{:S(2)}) copy-start(bf16[64,3072]{1,0:T(8,128)(2,1)} %param.33) | copy-start | bytes 1179652
  44.5 1.3 copy-start.2
  44.5 2.1 copy-start.10
  44.5 2.5 copy-start.15
  44.5 2.5 copy-start.17
  47.2 3.8 %copy-start.12 = (bf16[128,64]{0,1:T(8,128)(2,1)S(1)}, bf16[128,64]{0,1:T(8,128)(2,1)}, u32[]{:S(2)}) copy-start(bf16[128,64]{0,1:T(8,128)(2,1)} %param.44) | copy-start | bytes 49156
  47.2 3.8 %copy-start.20 = (f32[64]{0:T(128)S(1)}, f32[64]{0:T(128)}, u32[]{:S(2)}) copy-start(f32[64]{0:T(128)} %param.45) | copy-start | bytes 772
  47.2 4.0 %copy-start.11 = (bf16[64,64]{1,0:T(8,128)(2,1)S(1)}, bf16[64,64]{1,0:T(8,128)(2,1)}, u32[]{:S(2)}) copy-start(bf16[64,64]{1,0:T(8,128)(2,1)} %param.46) | copy-start | bytes 24580
  56.1 11.2 %copy-start.1 = (bf16[64,3072]{1,0:T(8,128)(2,1)S(1)}, bf16[64,3072]{1,0:T(8,128)(2,1)}, u32[]{:S(2)}) copy-start(bf16[64,3072]{1,0:T(8,128)(2,1)} %param.38) | copy-start | bytes 1179652
  67.2 1.7 copy-start.5
  73.9 52.8 %copy-start.9 = (f32[64,1024]{1,0:T(8,128)S(1)}, f32[64,1024]{1,0:T(8,128)}, u32[]{:S(2)}) copy-start(f32[64,1024]{1,0:T(8,128)} %custom-call.2) | copy-start | bytes 786436
  119.7 79.2 %collective-permute-start.2 = (bf16[64,4,128]{2,1,0:T(4,128)(2,1)S(1)}, bf16[64,4,128]{2,1,0:T(4,128)(2,1)S(1)}, u32[]{:S(2)}, u32[]{:S(2)}) collective-permute-start(bf16[64,4,128]{2,1,0:T(4,128)(2,1)S(1)} %get-tuple-element.824), channel_id=1, source_target_pairs={{0,4},{4,8},{8,12},{12,16},{16,20},{20,24},{24,28},{1,5},{5,9},{9,... | collective-permute-start | bytes 196616 | tf_op jit(solution)/shard_map/ppermute | solution.py:13
  123.7 75.2 %collective-permute-start.3 = (bf16[64,4,128]{2,1,0:T(4,128)(2,1)S(1)}, bf16[64,4,128]{2,1,0:T(4,128)(2,1)S(1)}, u32[]{:S(2)}, u32[]{:S(2)}) collective-permute-start(bf16[64,4,128]{2,1,0:T(4,128)(2,1)S(1)} %get-tuple-element.825), channel_id=1, source_target_pairs={{4,0},{8,4},{12,8},{16,12},{20,16},{24,20},{28,24},{5,1},{9,5},{13... | collective-permute-start | bytes 196616 | tf_op jit(solution)/shard_map/ppermute | solution.py:13
  126.5 107.0 %all-reduce.7.cloned.1.call-start = ((), (), s32[]{:S(2)}) async-start(), calls=%async_computation.3 | async-start | bytes 333824 | tf_op jit(solution)/shard_map/psum | solution.py:266
  132.9 113.3 %copy-start.8 = (f32[64,1024]{1,0:T(8,128)S(1)}, f32[64,1024]{1,0:T(8,128)}, u32[]{:S(2)}) copy-start(f32[64,1024]{1,0:T(8,128)} %custom-call.3) | copy-start | bytes 786436
  199.8 46.0 %all-to-all-start.1 = ((bf16[64,3,4,128]{3,0,1,2:T(8,128)(2,1)}), bf16[64,3,4,128]{3,0,1,2:T(8,128)(2,1)S(1)}, u32[]{:S(2)}, u32[]{:S(2)}) async-start(bf16[64,3,4,128]{3,0,1,2:T(8,128)(2,1)} %copy.54), calls=%async_computation.1 | async-start | bytes 393216 | tf_op jit(solution)/shard_map/all_to_all | solution.py:258
  (6 other events, 5.6 us)
Sparse Core Ops, SparseCore 0:
  126.6 72.2 all-reduce.4
  201.9 31.4 all-reduce.6
